TPU v7x, 32 devices: a whole 2x2x4 slice. The times are simulated.
32 devices in a mesh: dp: 8 (over y, x, core), seq: 4 (over z).
Axes of the slice: x: 2, y: 2, z: 4, core: 2. Of those that a mesh axis runs over, the one named last changes fastest.
Arguments:
- tokens: bfloat16 [8, 1024, 1024], P('dp', 'seq'), may hold values from -6 to 6
- segments: int32 [8, 1024], P('dp'), may hold values from 0 to 6, as said below
- w_qkv: bfloat16 [1024, 3072], P('dp'), may hold values from -0.1875 to 0.1875
- w_attn_out: bfloat16 [1024, 1024], P('dp'), may hold values from -0.1875 to 0.1875
- w_in: bfloat16 [1024, 8192], P('dp'), may hold values from -0.1875 to 0.1875
- w_down: bfloat16 [4096, 1024], P('dp'), may hold values from -0.09375 to 0.09375
- s_qk: float32 [1024], replicated, may hold values from 1 to 1.8
- s_u: float32 [4096], replicated, may hold values from 0.5 to 2
- s_v: float32 [4096], replicated, may hold values from 0.5 to 2
- alpha_attn: float32 [1024], replicated, may hold values from 0.05 to 0.4
- alpha_mlp: float32 [1024], replicated, may hold values from 0.05 to 0.4
- cotangent: bfloat16 [8, 1024, 1024], P('dp', 'seq'), may hold values from -6 to 6
Outputs:
- output: bfloat16 [8, 1024, 1024], P('dp', 'seq')
- grad_tokens: float32 [8, 1024, 1024], P('dp', 'seq')
- grad_w_qkv: float32 [1024, 3072], P(('dp', 'seq'))
- grad_w_attn_out: float32 [1024, 1024], P(('dp', 'seq'))
- grad_w_in: float32 [1024, 8192], P(('dp', 'seq'))
- grad_w_down: float32 [4096, 1024], P(('dp', 'seq'))
- grad_s_qk: float32 [1024], P(('dp', 'seq'))
- grad_s_u: float32 [4096], P(('dp', 'seq'))
- grad_s_v: float32 [4096], P(('dp', 'seq'))
- grad_alpha_attn: float32 [1024], P(('dp', 'seq'))
- grad_alpha_mlp: float32 [1024], P(('dp', 'seq'))
Inputs may be any that keep to these rules, and one draw needn't show every extreme that they name: `segments`: in each sequence ids count documents from 1 at the first token and rise by one at each new document; documents hold 200 to 2000 tokens except where a sequence's end cuts one; each sequence ends in 1 to 199 padding tokens of id 0; in one sequence of each draw every whole document holds exactly 200 tokens and one padding token ends it.
All inputs are finite; a program needn't handle non-finite values.
Results may differ from a plain program's by a relative error of at most 0.019.
Values may be sent and summed in bfloat16 or wider, within the bound.
A program may use at most 192 MiB of HBM per device.

v0:
```python
import math
import jax
import jax.numpy as jnp
from jax import lax
from jax.sharding import PartitionSpec as P

HEADS = 16
HD = 64
EPS = 1e-06
ROPE_BASE = 10000.0
MASKED_SCORE = -1e30


def as_sent(array):

    def short(part):
        return part.astype(jnp.bfloat16) if part.dtype == jnp.float32 else part

    return jax.tree.map(short, array)


def rms_norm(values):
    inverse = lax.rsqrt(jnp.mean(values * values, axis=-1, keepdims=True) + EPS)
    return (values * inverse, inverse)


def rms_back(grad_in, normed, inverse):
    return inverse * (grad_in - normed * jnp.mean(grad_in * normed, axis=-1, keepdims=True))


def contract_rows(left_arr, right_arr):
    return lax.dot_general(
        left_arr, right_arr, (((0,), (0,)), ((), ())), preferred_element_type=jnp.float32
    )


def contract_cols(left_arr, right_arr):
    return lax.dot_general(
        left_arr, right_arr, (((1,), (1,)), ((), ())), preferred_element_type=jnp.float32
    )


def doc_positions(seg_row):
    length = seg_row.shape[0]
    places = jnp.arange(length, dtype=jnp.int32)
    is_start = jnp.concatenate([jnp.ones((1,), dtype=bool), seg_row[1:] != seg_row[:-1]])
    starts = lax.cummax(jnp.where(is_start, places, 0), axis=0)
    return (places - starts).astype(jnp.float32)


def rope_tables(positions, head_dim):
    half_dim = head_dim // 2
    inverse_freq = ROPE_BASE ** (-(jnp.arange(half_dim, dtype=jnp.float32) * 2.0 / head_dim))
    angles = positions[:, None] * inverse_freq[None, :]
    return (jnp.cos(angles)[:, None, :], jnp.sin(angles)[:, None, :])


def rotate(values, cosine, sine_tab):
    half_dim = values.shape[-1] // 2
    low_half = values[..., :half_dim]
    high_half = values[..., half_dim:]
    return jnp.concatenate(
        [low_half * cosine - high_half * sine_tab, high_half * cosine + low_half * sine_tab],
        axis=-1,
    )


def head_prep(head_raw, cosine, sine_tab, head_gain):
    rotated = rotate(head_raw.astype(jnp.float32), cosine, sine_tab)
    head_unit, inverse = rms_norm(rotated)
    return (head_unit, inverse, (head_unit * head_gain).astype(jnp.bfloat16))


def head_back(grad_n, head_unit, inverse, head_gain, cosine, sine_tab):
    grad_rot = rms_back(grad_n * head_gain, head_unit, inverse)
    return rotate(grad_rot, cosine, -sine_tab)


def allowed(seg_row, block_start, block_len):
    query_idx = block_start + jnp.arange(block_len, dtype=jnp.int32)
    key_idx = jnp.arange(seg_row.shape[0], dtype=jnp.int32)
    seg_query = lax.dynamic_slice_in_dim(seg_row, block_start, block_len)
    same_doc = seg_query[:, None] == seg_row[None, :]
    causal = key_idx[None, :] <= query_idx[:, None]
    not_padding = (seg_query[:, None] != 0) | (key_idx[None, :] == query_idx[:, None])
    return causal & same_doc & not_padding


def attend_forward(query_n, key_n, value_b, seg_row, score_scale):
    length, groups, head_dim = query_n.shape
    block_len = min(512, length)
    block_count = length // block_len
    query_blocks = query_n.reshape(block_count, block_len, groups, head_dim)
    starts = jnp.arange(block_count, dtype=jnp.int32) * block_len

    def one_block(block_in):
        query_part, block_start = block_in
        scores = (
            jnp.einsum("qhd,khd->hqk", query_part, key_n, preferred_element_type=jnp.float32)
            * score_scale
        )
        mask_ok = allowed(seg_row, block_start, block_len)
        scores = jnp.where(mask_ok[None], scores, MASKED_SCORE)
        row_max = jnp.max(scores, axis=-1, keepdims=True)
        weights_exp = jnp.exp(scores - row_max)
        row_total = jnp.sum(weights_exp, axis=-1, keepdims=True)
        attn_probs = (weights_exp / row_total).astype(jnp.bfloat16)
        attn_part = jnp.einsum(
            "hqk,khd->qhd", attn_probs, value_b, preferred_element_type=jnp.float32
        )
        return (attn_part.astype(jnp.bfloat16), (row_max + jnp.log(row_total))[..., 0])

    attn_mixed, log_sums = lax.map(one_block, (query_blocks, starts))
    return (attn_mixed.reshape(length, groups * head_dim), log_sums)


def attend_backward(query_n, key_n, value_b, grad_attn, log_sums, seg_row, score_scale):
    length, groups, head_dim = query_n.shape
    block_len = min(512, length)
    block_count = length // block_len
    query_blocks = query_n.reshape(block_count, block_len, groups, head_dim)
    grad_blocks = grad_attn.reshape(block_count, block_len, groups, head_dim)
    starts = jnp.arange(block_count, dtype=jnp.int32) * block_len

    def one_block(accums, block_in):
        key_acc, value_acc = accums
        query_part, grad_part, lse_part, block_start = block_in
        scores = (
            jnp.einsum("qhd,khd->hqk", query_part, key_n, preferred_element_type=jnp.float32)
            * score_scale
        )
        mask_ok = allowed(seg_row, block_start, block_len)
        attn_probs = jnp.where(mask_ok[None], jnp.exp(scores - lse_part[..., None]), 0.0)
        grad_probs = jnp.einsum(
            "qhd,khd->hqk", grad_part, value_b, preferred_element_type=jnp.float32
        )
        delta_row = jnp.sum(grad_probs * attn_probs, axis=-1, keepdims=True)
        grad_scores = (attn_probs * (grad_probs - delta_row)).astype(jnp.bfloat16)
        grad_query = (
            jnp.einsum("hqk,khd->qhd", grad_scores, key_n, preferred_element_type=jnp.float32)
            * score_scale
        )
        key_acc = (
            key_acc
            + jnp.einsum(
                "hqk,qhd->khd", grad_scores, query_part, preferred_element_type=jnp.float32
            )
            * score_scale
        )
        value_acc = value_acc + jnp.einsum(
            "hqk,qhd->khd",
            attn_probs.astype(jnp.bfloat16),
            grad_part,
            preferred_element_type=jnp.float32,
        )
        return ((key_acc, value_acc), grad_query)

    zeros_init = jnp.zeros((length, groups, head_dim), jnp.float32)
    (grad_key, grad_value), grad_query = lax.scan(
        one_block, (zeros_init, zeros_init), (query_blocks, grad_blocks, log_sums, starts)
    )
    return (grad_query.reshape(length, groups, head_dim), grad_key, grad_value)


def body(
    tokens,
    segments,
    w_qkv,
    w_attn_out,
    w_in,
    w_down,
    s_qk,
    s_u,
    s_v,
    alpha_attn,
    alpha_mlp,
    cotangent,
):
    model_width = tokens.shape[-1]
    inputs_b = tokens.reshape(-1, model_width)
    inputs_f = inputs_b.astype(jnp.float32)
    seg_row = segments.reshape(-1)
    seq_count = lax.axis_size("seq")
    dp_count = lax.axis_size("dp")
    head_group = HEADS // seq_count
    group_width = head_group * HD
    offset = lax.axis_index("seq") * group_width
    head_gain = lax.dynamic_slice_in_dim(s_qk, offset, group_width).reshape(head_group, HD)
    score_scale = 1.0 / math.sqrt(HD)
    full_qkv, full_out, full_in, full_down = (
        lax.all_gather(w_qkv, "dp", axis=0, tiled=True),
        lax.all_gather(w_attn_out, "dp", axis=0, tiled=True),
        lax.all_gather(w_in, "dp", axis=0, tiled=True),
        lax.all_gather(w_down, "dp", axis=0, tiled=True),
    )
    projected = jnp.dot(inputs_b, full_qkv, preferred_element_type=jnp.float32).astype(jnp.bfloat16)
    by_heads = lax.all_to_all(
        projected.reshape(-1, 3, model_width), "seq", split_axis=2, concat_axis=0, tiled=True
    )
    length = by_heads.shape[0]
    cosine, sine_tab = rope_tables(doc_positions(seg_row), HD)
    query_unit, query_inv, query_n = head_prep(
        by_heads[:, 0].reshape(length, head_group, HD), cosine, sine_tab, head_gain
    )
    key_unit, key_inv, key_n = head_prep(
        by_heads[:, 1].reshape(length, head_group, HD), cosine, sine_tab, head_gain
    )
    value_b = by_heads[:, 2].reshape(length, head_group, HD)
    attn_mixed, log_sums = attend_forward(query_n, key_n, value_b, seg_row, score_scale)
    attn_pieces = lax.all_to_all(attn_mixed, "seq", split_axis=0, concat_axis=1, tiled=True)
    attn_proj = jnp.dot(attn_pieces, full_out, preferred_element_type=jnp.float32)
    attn_unit, attn_inv = rms_norm(attn_proj)
    hidden, hidden_inv = rms_norm(inputs_f + alpha_attn * (attn_unit - inputs_f))
    hidden_b = hidden.astype(jnp.bfloat16)
    up_gate = jnp.dot(hidden_b, full_in, preferred_element_type=jnp.float32)
    ff_width = s_u.shape[0]
    up_raw = up_gate[:, :ff_width]
    gate_raw = up_gate[:, ff_width:]
    up_val = s_u * up_raw
    gate_val = s_v * gate_raw
    gate_sig = jax.nn.sigmoid(gate_val)
    silu_gate = gate_val * gate_sig
    inner_act = (silu_gate * up_val).astype(jnp.bfloat16)
    down_proj = jnp.dot(inner_act, full_down, preferred_element_type=jnp.float32)
    mlp_unit, mlp_inv = rms_norm(down_proj)
    result, result_inv = rms_norm(hidden + alpha_mlp * (mlp_unit - hidden))
    output = result.astype(jnp.bfloat16).reshape(tokens.shape)
    grad_res = cotangent.reshape(-1, model_width).astype(jnp.float32)
    grad_two = rms_back(grad_res, result, result_inv)
    grad_alpha_mlp = jnp.sum(grad_two * (mlp_unit - hidden), axis=0)
    grad_down_proj = rms_back(alpha_mlp * grad_two, mlp_unit, mlp_inv).astype(jnp.bfloat16)
    grad_w_down = contract_rows(inner_act, grad_down_proj)
    grad_inner = contract_cols(grad_down_proj, full_down)
    grad_up_val = grad_inner * silu_gate
    grad_gate_val = grad_inner * up_val * gate_sig * (1.0 + gate_val * (1.0 - gate_sig))
    grad_s_u = jnp.sum(grad_up_val * up_raw, axis=0)
    grad_s_v = jnp.sum(grad_gate_val * gate_raw, axis=0)
    grad_up_gate = jnp.concatenate([grad_up_val * s_u, grad_gate_val * s_v], axis=1).astype(
        jnp.bfloat16
    )
    grad_w_in = contract_rows(hidden_b, grad_up_gate)
    grad_hidden = (1.0 - alpha_mlp) * grad_two + contract_cols(grad_up_gate, full_in)
    grad_one = rms_back(grad_hidden, hidden, hidden_inv)
    grad_alpha_attn = jnp.sum(grad_one * (attn_unit - inputs_f), axis=0)
    grad_attn_proj = rms_back(alpha_attn * grad_one, attn_unit, attn_inv).astype(jnp.bfloat16)
    grad_w_attn_out = contract_rows(attn_pieces, grad_attn_proj)
    grad_pieces = contract_cols(grad_attn_proj, full_out).astype(jnp.bfloat16)
    grad_heads = lax.all_to_all(
        grad_pieces, "seq", split_axis=1, concat_axis=0, tiled=True
    ).reshape(length, head_group, HD)
    grad_query_n, grad_key_n, grad_value = attend_backward(
        query_n, key_n, value_b, grad_heads, log_sums, seg_row, score_scale
    )
    grad_head_gain = jnp.sum(grad_query_n * query_unit + grad_key_n * key_unit, axis=0)
    grad_query = head_back(grad_query_n, query_unit, query_inv, head_gain, cosine, sine_tab)
    grad_key = head_back(grad_key_n, key_unit, key_inv, head_gain, cosine, sine_tab)
    grad_stack = (
        jnp.stack([grad_query, grad_key, grad_value], axis=1)
        .reshape(length, 3, group_width)
        .astype(jnp.bfloat16)
    )
    grad_qkv = lax.all_to_all(grad_stack, "seq", split_axis=0, concat_axis=2, tiled=True).reshape(
        -1, 3 * model_width
    )
    grad_w_qkv = contract_rows(inputs_b, grad_qkv)
    grad_inputs = (1.0 - alpha_attn) * grad_one + contract_cols(grad_qkv, full_qkv)
    grad_s_qk = lax.dynamic_update_slice_in_dim(
        jnp.zeros((model_width,), jnp.float32), grad_head_gain.reshape(-1), offset, 0
    )
    grad_terms = (
        grad_w_qkv,
        grad_w_attn_out,
        grad_w_in,
        grad_w_down,
        grad_s_qk,
        grad_s_u,
        grad_s_v,
        grad_alpha_attn,
        grad_alpha_mlp,
    )
    shaped = tuple(
        (
            term_arr.reshape(
                (dp_count, seq_count, term_arr.shape[0] // (dp_count * seq_count))
                + term_arr.shape[1:]
            )
            for term_arr in grad_terms
        )
    )
    within = jax.tree.map(
        lambda part: part.astype(jnp.float32),
        lax.psum_scatter(as_sent(shaped), "seq", scatter_dimension=1, tiled=True),
    )
    across = jax.tree.map(
        lambda part: part.astype(jnp.float32),
        lax.psum_scatter(as_sent(within), "dp", scatter_dimension=0, tiled=True),
    )
    shards = tuple((term_arr.reshape(term_arr.shape[2:]) for term_arr in across))
    return (output, grad_inputs.reshape(tokens.shape)) + tuple(shards)


def solution(mesh):
    placed = (
        P("dp", "seq", None),
        P("dp", None),
        P("dp", None),
        P("dp", None),
        P("dp", None),
        P("dp", None),
        P(),
        P(),
        P(),
        P(),
        P(),
        P("dp", "seq", None),
    )
    return jax.shard_map(
        body,
        mesh=mesh,
        in_specs=placed,
        out_specs=(
            P("dp", "seq", None),
            P("dp", "seq", None),
            P(("dp", "seq"), None),
            P(("dp", "seq"), None),
            P(("dp", "seq"), None),
            P(("dp", "seq"), None),
            P(("dp", "seq")),
            P(("dp", "seq")),
            P(("dp", "seq")),
            P(("dp", "seq")),
            P(("dp", "seq")),
        ),
        check_vma=False,
    )
```

profile of v0, /device:TPU:0, one launch (start us, length us, event | category | flops | bytes accessed | tf_op | source)
XLA Modules:
  0.0 1722.5 jit_solution(12970683820882381391)
XLA Ops:
  9.4 48.6 %all-gather.5.cloned.1.call-done = bf16[1024,3072]{1,0:T(8,128)(2,1)} async-done(((bf16[128,3072]{1,0:T(8,128)(2,1)}), bf16[1024,3072]{1,0:T(8,128)(2,1)}) %all-gather.5.cloned.1.call-update) | async-done | bytes 6291472 | tf_op jit(solution)/shard_map/all_gather | solution.py:191
  58.0 4.8 convolution_convert_fusion.3
  63.5 2.7 copy.92
  66.2 4.6 all-to-all-start
  74.2 45.2 %all-to-all-done = bf16[256,3,1024]{0,1,2:T(4,128)(2,1)S(1)} async-done(((bf16[256,3,1024]{0,1,2:T(4,128)(2,1)}), bf16[256,3,1024]{0,1,2:T(4,128)(2,1)S(1)}, u32[]{:S(2)}, u32[]{:S(2)}) %all-to-all-start) | async-done | bytes 1572896 | tf_op jit(solution)/shard_map/all_to_all | solution.py:197
  124.7 2.5 copy.96
  135.9 27.1 %while.27 = (s32[]{:T(128)}, bf16[2,512,4,64]{1,3,2,0:T(8,128)(2,1)}, f32[2,4,512]{2,1,0:T(4,128)S(1)}, s32[2]{0:T(128)S(1)}, s32[1024]{0:T(1024)S(1)}, /*index=...) while((s32[]{:T(128)}, ...), condition=%wide.region_7.8_spmd, body=%wide.region_4.7_spmd.sunk | while | flops 565312512 | bytes 33111288 | solution.py:113
  140.0 2.6 fusion.121
  145.0 3.7 fusion.123
  153.6 2.6 fusion.121
  158.6 3.7 fusion.123
  165.7 3.7 all-to-all-start.1
  169.5 13.9 all-to-all-done.1
  183.4 2.6 multiply_reduce_fusion.13
  187.5 9.0 fusion.72
  196.5 3.2 copy-done
  202.0 33.4 %all-gather.11.cloned.1.call-done = bf16[4096,1024]{1,0:T(8,128)(2,1)} async-done(((bf16[512,1024]{1,0:T(8,128)(2,1)}), bf16[4096,1024]{1,0:T(8,128)(2,1)}) %all-gather.11.cloned.1.call-update) | async-done | bytes 8388624 | tf_op jit(solution)/shard_map/all_gather | solution.py:194
  235.4 6.5 multiply_reduce_fusion.11
  245.9 9.2 multiply_reduce_fusion.1
  256.8 12.7 multiply_reduce_fusion.8
  269.6 2.9 multiply_reduce_fusion.4
  275.4 4.8 all-to-all-start.2
  280.2 14.9 all-to-all-done.2
  299.0 62.1 %while.28 = (s32[]{:T(128)}, f32[1024,4,64]{0,2,1:T(8,128)S(1)}, f32[1024,4,64]{0,2,1:T(8,128)}, f32[2,512,4,64]{1,0,3,2:T(2,128)}, bf16[2,512,4,64]{1,3,2,0:T(8...) while((s32[]{:T(128)}, f32[1024,4,64]{0,2,1:T(8,128)S(1)}, ...), condition=%wide.region_18.19_spmd.clone, body=%wide.region_16.18_spmd.clone.sunk | while | flops 1378221056 | bytes 82910512 | solution.py:159
  305.5 3.1 fusion.136
  308.6 4.8 multiply_reduce_fusion.17
  319.7 10.4 dynamic_update_slice.24
  336.5 3.1 fusion.136
  339.7 4.8 multiply_reduce_fusion.17
  350.7 10.4 dynamic_update_slice.24
  363.6 3.1 reshape.556
  371.1 2.6 copy.107
  373.8 4.6 all-to-all-start.3
  380.5 7.2 convolution_convert_fusion.1
  387.7 10.4 convolution_convert_fusion
  398.2 28.0 %all-to-all-done.3 = bf16[1024,3,256]{2,1,0:T(4,128)(2,1)} async-done(((bf16[1024,3,256]{2,1,0:T(4,128)(2,1)}), bf16[1024,3,256]{2,1,0:T(4,128)(2,1)}, u32[]{:S(2)}, u32[]{:S(2)}) %all-to-all-start.3) | async-done | bytes 1572896 | tf_op jit(solution)/shard_map/all_to_all | solution.py:262
  428.7 5.5 convolution_convert_fusion.2
  435.5 1101.0 %all-reduce.19.cloned.1.call-done = (bf16[8,4,32,3072]{3,2,1,0:T(8,128)(2,1)}, bf16[8,4,32,1024]{3,2,1,0:T(8,128)(2,1)}, bf16[8,4,32,8192]{3,2,1,0:T(8,128)(2,1)}, bf16[8,4,128,1024]{3,2,1,0:T(8,128)(2,1)}) async-done(((bf16[8,4,32,3072]{3,2,1,0:T(8,128)(2,1)}, bf16[8,4,32,1024]{3,2,1,0:T(8,128)(2,1)}, bf16[8,4,32,8192]{3,2,1,0:T(8,128)(2,1)}, bf16[8,4,128,1024]{3,2,1,0:T(8,128)(2,1)}), ...) | async-done | bytes 33554448
  1536.4 2.5 constant_dynamic-slice_fusion.12
  1539.0 3.3 constant_dynamic-slice_fusion.13
  1542.4 3.8 constant_dynamic-slice_fusion.10
  1546.5 5.3 constant_dynamic-slice_fusion.11
  1553.7 16.8 all-reduce.15
  1573.8 22.4 %all-reduce.14 = (bf16[8,1,32]{2,1,0:T(2,128)(2,1)S(1)}, bf16[8,1,128]{2,1,0:T(2,128)(2,1)S(1)}, bf16[8,1,128]{2,1,0:T(2,128)(2,1)S(1)}, bf16[8,1,32]{2,1,0:T(2,128)(2,1)S(1)}, bf16[8,1,32]{2,1,0:T(2,128)(2,1)S(1)}) all-reduce(bf16[8,1,32]{2,1,0:T(2,128)(2,1)S(1)} %copy.111, ...), channel_id=11, replica_groups=mesh['dp'=8,'seq'=4] {'dp'}, use_global_device_ids=true, to_apply=%region_31.32.clone | all-reduce | flops 2816 | bytes 11264
  1602.0 5.7 fusion.50
  1609.2 5.4 reduce-scatter.17.cloned.1.call-done
  1616.3 42.7 %reduce-scatter.23.cloned.1.call-done = bf16[1,1,128,1024]{3,2,1,0:T(8,128)(2,1)} async-done(((bf16[8,1,128,1024]{3,2,1,0:T(8,128)(2,1)}), bf16[1,1,128,1024]{3,2,1,0:T(8,128)(2,1)}) %reduce-scatter.23.cloned.1.call-update) | async-done | bytes 262160 | tf_op jit(solution)/shard_map/reduce_scatter | solution.py:296
  1660.8 52.8 %reduce-scatter.21.cloned.1.call-done = bf16[1,1,32,8192]{3,2,1,0:T(8,128)(2,1)} async-done(((bf16[8,1,32,8192]{3,2,1,0:T(8,128)(2,1)}), bf16[1,1,32,8192]{3,2,1,0:T(8,128)(2,1)}) %reduce-scatter.21.cloned.1.call-update) | async-done | bytes 524304 | tf_op jit(solution)/shard_map/reduce_scatter | solution.py:296
  (263 shorter events, 102.1 us)
Async XLA Ops:
  7.2 50.8 %all-gather.5.cloned.1.call-start = ((), (), s32[]{:S(2)}) async-start(), calls=%async_computation.8 | async-start | bytes 7077888 | tf_op jit(solution)/shard_map/all_gather | solution.py:191
  7.9 161.6 %all-gather.7.cloned.1.call-start = ((), (), s32[]{:S(2)}) async-start(), calls=%async_computation.9 | async-start | bytes 2359296 | tf_op jit(solution)/shard_map/all_gather | solution.py:192
  8.7 178.8 %all-gather.9.cloned.1.call-start = ((), (), s32[]{:S(2)}) async-start(), calls=%async_computation.10 | async-start | bytes 18874368 | tf_op jit(solution)/shard_map/all_gather | solution.py:193
  63.5 8.8 copy-start.22
  66.2 53.2 %all-to-all-start = ((bf16[256,3,1024]{0,1,2:T(4,128)(2,1)}), bf16[256,3,1024]{0,1,2:T(4,128)(2,1)S(1)}, u32[]{:S(2)}, u32[]{:S(2)}) async-start(bf16[256,3,1024]{0,1,2:T(4,128)(2,1)} %copy.92), calls=%async_computation | async-start | bytes 4194304 | tf_op jit(solution)/shard_map/all_to_all | solution.py:197
  70.8 164.6 %all-gather.11.cloned.1.call-start = ((), (), s32[]{:S(2)}) async-start(), calls=%async_computation.11 | async-start | bytes 9437184 | tf_op jit(solution)/shard_map/all_gather | solution.py:194
  72.3 61.1 %copy-start.36 = (f32[4,64]{1,0:T(4,128)}, f32[4,64]{1,0:T(4,128)S(1)}, u32[]{:S(2)}) copy-start(f32[4,64]{1,0:T(4,128)S(1)} %mul.496) | copy-start | bytes 3076
  74.2 54.3 %copy-start.23 = (f32[1024,32]{0,1:T(8,128)}, f32[1024,32]{0,1:T(8,128)S(1)}, u32[]{:S(2)}) copy-start(f32[1024,32]{0,1:T(8,128)S(1)} %get-tuple-element.371) | copy-start | bytes 393220
  130.5 5.4 copy-start.4
  130.5 5.4 copy-start.6
  130.5 5.4 copy-start.8
  130.6 5.3 copy-start.9
  131.0 4.9 copy-start.11
  133.3 2.6 copy-start.34
  133.4 2.6 copy-start.32
  163.0 6.4 copy-start.39
  163.0 23.9 %copy-start.10 = (bf16[1,256,1024]{2,1,0:T(8,128)(2,1)S(1)}, bf16[1,256,1024]{2,1,0:T(8,128)(2,1)}, u32[]{:S(2)}) copy-start(bf16[1,256,1024]{2,1,0:T(8,128)(2,1)} %param.16) | copy-start | bytes 1572868
  163.0 23.9 %copy-start.40 = (f32[1024]{0:T(1024)S(1)}, f32[1024]{0:T(1024)}, u32[]{:S(2)}) copy-start(f32[1024]{0:T(1024)} %param.25) | copy-start | bytes 12292
  165.7 17.6 %all-to-all-start.1 = ((bf16[4,256,256]{1,2,0:T(8,128)(2,1)}), bf16[4,256,256]{1,2,0:T(8,128)(2,1)S(1)}, u32[]{:S(2)}, u32[]{:S(2)}) async-start(bf16[4,256,256]{1,2,0:T(8,128)(2,1)} %copy.100), calls=%async_computation.1 | async-start | bytes 1048576 | tf_op jit(solution)/shard_map/all_to_all | solution.py:210
  183.4 2.6 copy-start.13
  187.5 12.3 copy-start.38
  187.5 12.3 copy-start.42
  196.5 3.2 copy-start
  235.4 7.0 copy-start.12
  242.4 3.6 copy-start.1
  245.0 10.1 copy-start.17
  269.6 2.9 copy-start.3
  269.6 4.0 copy-start.19
  272.4 7.8 copy-start.15
  275.4 19.7 %all-to-all-start.2 = ((bf16[256,4,256]{0,2,1:T(8,128)(2,1)}), bf16[256,4,256]{0,2,1:T(8,128)(2,1)S(1)}, u32[]{:S(2)}, u32[]{:S(2)}) async-start(bf16[256,4,256]{0,2,1:T(8,128)(2,1)} %bitcast.275), calls=%async_computation.2 | async-start | bytes 1048576 | tf_op jit(solution)/shard_map/all_to_all | solution.py:248
  299.0 62.1 %copy-start.33 = (f32[2,512,4]{1,0,2:T(2,128)S(1)}, f32[2,512,4]{1,0,2:T(2,128)}, u32[]{:S(2)}) copy-start(f32[2,512,4]{1,0,2:T(2,128)} %copy-done.32) | copy-start | bytes 49156
  299.0 62.1 %copy-start.37 = (f32[4,64]{1,0:T(4,128)S(1)}, f32[4,64]{1,0:T(4,128)}, u32[]{:S(2)}) copy-start(f32[4,64]{1,0:T(4,128)} %copy-done.36) | copy-start | bytes 3076
  308.6 4.8 copy-start.26
  339.6 4.8 copy-start.26
  361.1 6.9 copy-start.5
  361.1 6.9 copy-start.7
  361.1 6.9 copy-start.31
  361.1 6.9 copy-start.35
  371.1 7.3 copy-start.14
  373.8 4.7 copy-start.21
  373.8 6.7 copy-start.18
  373.8 52.4 %all-to-all-start.3 = ((bf16[1024,3,256]{2,1,0:T(4,128)(2,1)}), bf16[1024,3,256]{2,1,0:T(4,128)(2,1)}, u32[]{:S(2)}, u32[]{:S(2)}) async-start(bf16[1024,3,256]{2,1,0:T(4,128)(2,1)} %copy.107), calls=%async_computation.3 | async-start | bytes 4194304 | tf_op jit(solution)/shard_map/all_to_all | solution.py:262
  378.4 1158.0 %all-reduce.19.cloned.1.call-start = ((), (), s32[]{:S(2)}) async-start(), calls=%async_computation.16 | async-start | bytes 67108864
  434.2 1173.5 %reduce-scatter.19.cloned.1.call-start = ((), (), s32[]{:S(2)}) async-start(), calls=%async_computation.13 | async-start | bytes 589824 | tf_op jit(solution)/shard_map/reduce_scatter | solution.py:296
  1539.0 75.7 %reduce-scatter.17.cloned.1.call-start = ((), (), s32[]{:S(2)}) async-start(), calls=%async_computation.12 | async-start | bytes 1769472 | tf_op jit(solution)/shard_map/reduce_scatter | solution.py:296
  1542.3 116.7 %reduce-scatter.23.cloned.1.call-start = ((), (), s32[]{:S(2)}) async-start(), calls=%async_computation.15 | async-start | bytes 2359296 | tf_op jit(solution)/shard_map/reduce_scatter | solution.py:296
  1546.2 167.4 %reduce-scatter.21.cloned.1.call-start = ((), (), s32[]{:S(2)}) async-start(), calls=%async_computation.14 | async-start | bytes 4718592 | tf_op jit(solution)/shard_map/reduce_scatter | solution.py:296
  1551.9 50.1 %copy-start.16 = (f32[256,1024]{1,0:T(8,128)S(1)}, f32[256,1024]{1,0:T(8,128)}, u32[]{:S(2)}) copy-start(f32[256,1024]{1,0:T(8,128)} %copy-done.15) | copy-start | bytes 3145732
  (18 other events, 26.1 us)
Sparse Core Ops, SparseCore 0:
  9.9 48.1 all-gather.4
  59.9 27.7 all-gather.6
  89.6 89.7 all-gather.8
  181.1 54.2 all-gather.10
  434.4 1102.0 all-reduce.18
  1539.9 33.0 reduce-scatter.18
  1576.3 38.3 reduce-scatter.16
  1617.9 41.0 reduce-scatter.22
  1662.4 51.1 reduce-scatter.20
where the time goes:
time: 1730 us; the launch traced here: 1720 us
  waiting for transfers between devices  1390 us (80%)
  matrix products  116 us (7%)
  local copies, waits for them, and re-layouts  84.5 us (5%)
  other arithmetic  52.8 us (3%)
  blocking collectives  39.2 us (2%)
  starting transfers between devices  18.4 us (1%)
    unnamed x10, waiting for transfers between devices  1100 us
    reduce_scatter x4, waiting for transfers between devices, body(): lax.psum_scatter(as_sent(within), 'dp', scatter_dimension=0, tiled=True)  101 us
    all_gather x1, waiting for transfers between devices, body(): lax.all_gather(w_qkv, 'dp', axis=0, tiled=True)  48.6 us
    all_to_all x1, waiting for transfers between devices, body(): lax.all_to_all(projected.reshape(-1, 3, model_width), 'seq', split_axis=2...  45.2 us
    unnamed x2, blocking collectives  39.2 us
  transfers between devices with their start and end apart: 13, of which 10 were waited for; matrix products, arithmetic and copies ran while one was open for 7% of the time, Pallas kernels for 0%

commit v1 on v0

--- a/solution.py
+++ b/solution.py
@@ -187,8 +187,36 @@
     offset = lax.axis_index("seq") * group_width
     head_gain = lax.dynamic_slice_in_dim(s_qk, offset, group_width).reshape(head_group, HD)
     score_scale = 1.0 / math.sqrt(HD)
+
+    def gates_do(mesh_dim, vector):
+        runs = []
+        seen_now, k_now, odd = (lax.axis_size(mesh_dim), lax.axis_index(mesh_dim), vector.shape[0])
+        for c, u in enumerate(vector.shape):
+            runs.append(u * seen_now if c == 0 else u)
+        tall = opened = vector
+        local_next = lax.dynamic_update_slice_in_dim(
+            jnp.zeros(runs, vector.dtype), vector, k_now * odd, axis=0
+        )
+        for i in tuple(range(1, seen_now // 2 + 1)):
+            so_far_all = []
+            for c in tuple(range(seen_now)):
+                so_far_all.append((c, (c + 1) % seen_now))
+            tall = lax.ppermute(tall, axis_name=mesh_dim, perm=so_far_all)
+            local_next = lax.dynamic_update_slice_in_dim(
+                local_next, tall, (k_now - i) % seen_now * odd, axis=0
+            )
+            if 2 * i < seen_now:
+                copies = []
+                for c in [*range(seen_now)]:
+                    copies.append((c, (c - 1) % seen_now))
+                opened = lax.ppermute(opened, mesh_dim, copies)
+                local_next = lax.dynamic_update_slice_in_dim(
+                    local_next, opened, (k_now + i) % seen_now * odd, axis=0
+                )
+        return local_next
+
     full_qkv, full_out, full_in, full_down = (
-        lax.all_gather(w_qkv, "dp", axis=0, tiled=True),
+        gates_do("dp", w_qkv),
         lax.all_gather(w_attn_out, "dp", axis=0, tiled=True),
         lax.all_gather(w_in, "dp", axis=0, tiled=True),
         lax.all_gather(w_down, "dp", axis=0, tiled=True),

time: 1730 us -> 1740 us (level)
  starting transfers between devices: 18.4 us -> 41 us
  waiting for transfers between devices: 1390 us -> 1370 us
    ppermute x0 -> x7, waiting for transfers between devices: none -> 67.2 us  [the longest x4 63.5 us: gates_do(): tall = lax.ppermute(tall, axis_name=mesh_dim, perm=so_far_all)]
    all_gather x1 -> x0, waiting for transfers between devices: 48.6 us -> none  [body(): lax.all_gather(w_qkv, 'dp', axis=0, tiled=True)]
    all_gather x1, waiting for transfers between devices: 33.4 us -> 0.01 us  [body(): lax.all_gather(w_down, 'dp', axis=0, tiled=True)]
    ppermute x0 -> x7, starting transfers between devices: none -> 19.1 us  [the longest x4 11.9 us: gates_do(): tall = lax.ppermute(tall, axis_name=mesh_dim, perm=so_far_all)]
    unnamed x10 -> x9, waiting for transfers between devices: 1100 us -> 1110 us
  transfers between devices with their start and end apart: 13 -> 19, of which waited for: 10 -> 14; matrix products, arithmetic and copies ran while one was open for 7% -> 7% of each run, Pallas kernels for 0% -> 0%
where the time goes in v1:
time: 1740 us
  waiting for transfers between devices  1370 us (79%)
  matrix products  115 us (7%)
  local copies, waits for them, and re-layouts  95.4 us (5%)
  other arithmetic  50.4 us (3%)
  starting transfers between devices  41 us (2%)
  blocking collectives  39.2 us (2%)
    unnamed x9, waiting for transfers between devices  1110 us
    reduce_scatter x4, waiting for transfers between devices, body(): lax.psum_scatter(as_sent(within), 'dp', scatter_dimension=0, tiled=True)  101 us
    ppermute x4, waiting for transfers between devices, gates_do(): tall = lax.ppermute(tall, axis_name=mesh_dim, perm=so_far_all)  63.5 us
    all_to_all x1, waiting for transfers between devices, body(): lax.all_to_all(projected.reshape(-1, 3, model_width), 'seq', split_axis=2...  40.1 us
    unnamed x2, blocking collectives  39.2 us
  transfers between devices with their start and end apart: 19, of which 14 were waited for; matrix products, arithmetic and copies ran while one was open for 7% of the time, Pallas kernels for 0%

profile of v1, /device:TPU:0, one launch (start us, length us, event | category | flops | bytes accessed | tf_op | source)
XLA Modules:
  0.0 1735.7 jit_solution(18096262606027950302)
XLA Ops:
  9.2 2.9 collective-permute-start.1
  12.2 18.5 %collective-permute-done = bf16[128,3072]{1,0:T(8,128)(2,1)S(1)} collective-permute-done((bf16[128,3072]{1,0:T(8,128)(2,1)}, bf16[128,3072]{1,0:T(8,128)(2,1)S(1)}, u32[]{:S(2)}, u32[]{:S(2)}) %collective-permute-start) | collective-permute-done | bytes 786464 | tf_op jit(solution)/shard_map/ppermute | solution.py:204
  34.9 3.4 broadcast_in_dim.56
  39.2 15.3 collective-permute-done.2
  60.2 17.8 %collective-permute-done.4 = bf16[128,3072]{1,0:T(8,128)(2,1)S(1)} collective-permute-done((bf16[128,3072]{1,0:T(8,128)(2,1)S(1)}, bf16[128,3072]{1,0:T(8,128)(2,1)S(1)}, u32[]{:S(2)}, u32[]{:S(2)}) %collective-permute-start.4) | collective-permute-done | bytes 786464 | tf_op jit(solution)/shard_map/ppermute | solution.py:204
  78.0 9.4 collective-permute-start.6
  90.4 2.7 collective-permute-done.5
  94.1 12.0 collective-permute-done.6
  107.1 5.1 convolution_convert_fusion.3
  114.9 9.0 all-to-all-start
  127.5 40.1 %all-to-all-done = bf16[256,3,1024]{0,1,2:T(4,128)(2,1)S(1)} async-done(((bf16[256,3,1024]{0,1,2:T(4,128)(2,1)}), bf16[256,3,1024]{0,1,2:T(4,128)(2,1)S(1)}, u32[]{:S(2)}, u32[]{:S(2)}) %all-to-all-start) | async-done | bytes 1572896 | tf_op jit(solution)/shard_map/all_to_all | solution.py:225
  170.3 2.8 all_to_all.53
  181.2 27.1 %while.27 = (s32[]{:T(128)}, bf16[2,512,4,64]{1,3,2,0:T(8,128)(2,1)}, f32[2,4,512]{2,1,0:T(4,128)S(1)}, s32[2]{0:T(128)S(1)}, s32[1024]{0:T(1024)S(1)}, /*index=...) while((s32[]{:T(128)}, ...), condition=%wide.region_7.8_spmd, body=%wide.region_4.7_spmd.sunk | while | flops 565312512 | bytes 33111288 | solution.py:113
  190.3 3.7 fusion.123
  203.8 3.7 fusion.123
  211.0 3.9 all-to-all-start.1
  215.0 14.1 all-to-all-done.1
  233.2 8.2 fusion.72
  241.4 3.2 copy-done
  246.9 6.5 multiply_reduce_fusion.11
  257.4 8.8 multiply_reduce_fusion.1
  267.9 12.7 multiply_reduce_fusion.8
  280.7 2.9 multiply_reduce_fusion.4
  286.5 3.6 all-to-all-start.2
  290.2 14.0 all-to-all-done.2
  308.2 62.1 %while.28 = (s32[]{:T(128)}, f32[1024,4,64]{0,2,1:T(8,128)S(1)}, f32[1024,4,64]{0,2,1:T(8,128)}, f32[2,512,4,64]{1,0,3,2:T(2,128)}, bf16[2,512,4,64]{1,3,2,0:T(8...) while((s32[]{:T(128)}, f32[1024,4,64]{0,2,1:T(8,128)S(1)}, ...), condition=%wide.region_18.19_spmd.clone, body=%wide.region_16.18_spmd.clone.sunk | while | flops 1378221056 | bytes 82910512 | solution.py:159
  314.6 3.1 fusion.136
  317.7 4.8 multiply_reduce_fusion.17
  328.8 10.4 dynamic_update_slice.64
  345.7 3.1 fusion.136
  348.8 4.8 multiply_reduce_fusion.17
  359.9 10.4 dynamic_update_slice.64
  372.7 3.1 reshape.556
  382.9 4.6 all-to-all-start.3
  389.6 7.2 convolution_convert_fusion.1
  396.8 10.4 convolution_convert_fusion
  407.3 28.0 %all-to-all-done.3 = bf16[1024,3,256]{2,1,0:T(4,128)(2,1)} async-done(((bf16[1024,3,256]{2,1,0:T(4,128)(2,1)}), bf16[1024,3,256]{2,1,0:T(4,128)(2,1)}, u32[]{:S(2)}, u32[]{:S(2)}) %all-to-all-start.3) | async-done | bytes 1572896 | tf_op jit(solution)/shard_map/all_to_all | solution.py:290
  437.8 5.4 convolution_convert_fusion.2
  444.5 1105.0 %all-reduce.19.cloned.1.call-done = (bf16[8,4,32,3072]{3,2,1,0:T(8,128)(2,1)}, bf16[8,4,32,1024]{3,2,1,0:T(8,128)(2,1)}, bf16[8,4,32,8192]{3,2,1,0:T(8,128)(2,1)}, bf16[8,4,128,1024]{3,2,1,0:T(8,128)(2,1)}) async-done(((bf16[8,4,32,3072]{3,2,1,0:T(8,128)(2,1)}, bf16[8,4,32,1024]{3,2,1,0:T(8,128)(2,1)}, bf16[8,4,32,8192]{3,2,1,0:T(8,128)(2,1)}, bf16[8,4,128,1024]{3,2,1,0:T(8,128)(2,1)}), ...) | async-done | bytes 33554448
  1552.1 3.3 constant_dynamic-slice_fusion.13
  1555.4 3.8 constant_dynamic-slice_fusion.10
  1559.5 5.3 constant_dynamic-slice_fusion.11
  1566.6 16.8 all-reduce.15
  1586.8 22.4 %all-reduce.14 = (bf16[8,1,32]{2,1,0:T(2,128)(2,1)S(1)}, bf16[8,1,128]{2,1,0:T(2,128)(2,1)S(1)}, bf16[8,1,128]{2,1,0:T(2,128)(2,1)S(1)}, bf16[8,1,32]{2,1,0:T(2,128)(2,1)S(1)}, bf16[8,1,32]{2,1,0:T(2,128)(2,1)S(1)}) all-reduce(bf16[8,1,32]{2,1,0:T(2,128)(2,1)S(1)} %copy.90, ...), channel_id=11, replica_groups=mesh['dp'=8,'seq'=4] {'dp'}, use_global_device_ids=true, to_apply=%region_31.32.clone | all-reduce | flops 2816 | bytes 11264
  1615.0 5.7 fusion.50
  1622.2 5.4 reduce-scatter.17.cloned.1.call-done
  1629.3 42.7 %reduce-scatter.23.cloned.1.call-done = bf16[1,1,128,1024]{3,2,1,0:T(8,128)(2,1)} async-done(((bf16[8,1,128,1024]{3,2,1,0:T(8,128)(2,1)}), bf16[1,1,128,1024]{3,2,1,0:T(8,128)(2,1)}) %reduce-scatter.23.cloned.1.call-update) | async-done | bytes 262160 | tf_op jit(solution)/shard_map/reduce_scatter | solution.py:324
  1673.8 52.8 %reduce-scatter.21.cloned.1.call-done = bf16[1,1,32,8192]{3,2,1,0:T(8,128)(2,1)} async-done(((bf16[8,1,32,8192]{3,2,1,0:T(8,128)(2,1)}), bf16[1,1,32,8192]{3,2,1,0:T(8,128)(2,1)}) %reduce-scatter.21.cloned.1.call-update) | async-done | bytes 524304 | tf_op jit(solution)/shard_map/reduce_scatter | solution.py:324
  (281 shorter events, 129.7 us)
Async XLA Ops:
  7.2 207.8 %all-gather.4.cloned.1.call-start = ((), (), s32[]{:S(2)}) async-start(), calls=%async_computation.8 | async-start | bytes 2359296 | tf_op jit(solution)/shard_map/all_gather | solution.py:220
  7.9 30.4 %copy-start.26 = (bf16[128,3072]{1,0:T(8,128)(2,1)S(1)}, bf16[128,3072]{1,0:T(8,128)(2,1)}, u32[]{:S(2)}) copy-start(bf16[128,3072]{1,0:T(8,128)(2,1)} %param.18) | copy-start | bytes 2359300
  7.9 225.2 %all-gather.6.cloned.1.call-start = ((), (), s32[]{:S(2)}) async-start(), calls=%async_computation.9 | async-start | bytes 18874368 | tf_op jit(solution)/shard_map/all_gather | solution.py:221
  8.7 21.9 %collective-permute-start = (bf16[128,3072]{1,0:T(8,128)(2,1)}, bf16[128,3072]{1,0:T(8,128)(2,1)S(1)}, u32[]{:S(2)}, u32[]{:S(2)}) collective-permute-start(bf16[128,3072]{1,0:T(8,128)(2,1)} %param.18), channel_id=1, source_target_pairs={{0,4},{4,8},{8,12},{12,16},{16,20},{20,24},{24,28},{28,0},{1,5},{5... | collective-permute-start | bytes 2359304 | tf_op jit(solution)/shard_map/ppermute | solution.py:204
  9.2 23.0 %collective-permute-start.1 = (bf16[128,3072]{1,0:T(8,128)(2,1)}, bf16[128,3072]{1,0:T(8,128)(2,1)S(1)}, u32[]{:S(2)}, u32[]{:S(2)}) collective-permute-start(bf16[128,3072]{1,0:T(8,128)(2,1)} %param.18), channel_id=1, source_target_pairs={{0,28},{4,0},{8,4},{12,8},{16,12},{20,16},{24,20},{28,24},{1,29},{... | collective-permute-start | bytes 2359304 | tf_op jit(solution)/shard_map/ppermute | solution.py:212
  30.6 23.9 %collective-permute-start.2 = (bf16[128,3072]{1,0:T(8,128)(2,1)S(1)}, bf16[128,3072]{1,0:T(8,128)(2,1)S(1)}, u32[]{:S(2)}, u32[]{:S(2)}) collective-permute-start(bf16[128,3072]{1,0:T(8,128)(2,1)S(1)} %collective-permute-done), channel_id=1, source_target_pairs={{0,4},{4,8},{8,12},{12,16},{16,20},{20,24},{24,28},{28,0},{1,5},{5... | collective-permute-start | bytes 2359304 | tf_op jit(solution)/shard_map/ppermute | solution.py:204
  32.2 25.5 %collective-permute-start.3 = (bf16[128,3072]{1,0:T(8,128)(2,1)S(1)}, bf16[128,3072]{1,0:T(8,128)(2,1)}, u32[]{:S(2)}, u32[]{:S(2)}) collective-permute-start(bf16[128,3072]{1,0:T(8,128)(2,1)S(1)} %collective-permute-done.1), channel_id=1, source_target_pairs={{0,28},{4,0},{8,4},{12,8},{16,12},{20,16},{24,20},{28,24},{1,29},{... | collective-permute-start | bytes 2359304 | tf_op jit(solution)/shard_map/ppermute | solution.py:212
  54.5 23.5 %collective-permute-start.4 = (bf16[128,3072]{1,0:T(8,128)(2,1)S(1)}, bf16[128,3072]{1,0:T(8,128)(2,1)S(1)}, u32[]{:S(2)}, u32[]{:S(2)}) collective-permute-start(bf16[128,3072]{1,0:T(8,128)(2,1)S(1)} %collective-permute-done.2), channel_id=1, source_target_pairs={{0,4},{4,8},{8,12},{12,16},{16,20},{20,24},{24,28},{28,0},{1,5},{5... | collective-permute-start | bytes 2359304 | tf_op jit(solution)/shard_map/ppermute | solution.py:204
  57.7 49.4 %copy-start.10 = (bf16[1,256,1024]{2,1,0:T(8,128)(2,1)S(1)}, bf16[1,256,1024]{2,1,0:T(8,128)(2,1)}, u32[]{:S(2)}) copy-start(bf16[1,256,1024]{2,1,0:T(8,128)(2,1)} %param.16) | copy-start | bytes 1572868
  57.7 35.5 %collective-permute-start.5 = (bf16[128,3072]{1,0:T(8,128)(2,1)}, bf16[128,3072]{1,0:T(8,128)(2,1)S(1)}, u32[]{:S(2)}, u32[]{:S(2)}) collective-permute-start(bf16[128,3072]{1,0:T(8,128)(2,1)} %collective-permute-done.3), channel_id=1, source_target_pairs={{0,28},{4,0},{8,4},{12,8},{16,12},{20,16},{24,20},{28,24},{1,29},{... | collective-permute-start | bytes 2359304 | tf_op jit(solution)/shard_map/ppermute | solution.py:212
  78.0 28.2 %collective-permute-start.6 = (bf16[128,3072]{1,0:T(8,128)(2,1)S(1)}, bf16[128,3072]{1,0:T(8,128)(2,1)S(1)}, u32[]{:S(2)}, u32[]{:S(2)}) collective-permute-start(bf16[128,3072]{1,0:T(8,128)(2,1)S(1)} %collective-permute-done.4), channel_id=1, source_target_pairs={{0,4},{4,8},{8,12},{12,16},{16,20},{20,24},{24,28},{28,0},{1,5},{5... | collective-permute-start | bytes 2359304 | tf_op jit(solution)/shard_map/ppermute | solution.py:204
  112.2 13.4 copy-start.21
  114.9 52.7 %all-to-all-start = ((bf16[256,3,1024]{0,1,2:T(4,128)(2,1)}), bf16[256,3,1024]{0,1,2:T(4,128)(2,1)S(1)}, u32[]{:S(2)}, u32[]{:S(2)}) async-start(bf16[256,3,1024]{0,1,2:T(4,128)(2,1)} %copy.75), calls=%async_computation | async-start | bytes 4194304 | tf_op jit(solution)/shard_map/all_to_all | solution.py:225
  123.9 122.9 %all-gather.8.cloned.1.call-start = ((), (), s32[]{:S(2)}) async-start(), calls=%async_computation.10 | async-start | bytes 9437184 | tf_op jit(solution)/shard_map/all_gather | solution.py:222
  125.5 53.0 %copy-start.36 = (f32[4,64]{1,0:T(4,128)}, f32[4,64]{1,0:T(4,128)S(1)}, u32[]{:S(2)}) copy-start(f32[4,64]{1,0:T(4,128)S(1)} %mul.528) | copy-start | bytes 3076
  127.5 46.8 %copy-start.22 = (f32[1024,32]{0,1:T(8,128)}, f32[1024,32]{0,1:T(8,128)S(1)}, u32[]{:S(2)}) copy-start(f32[1024,32]{0,1:T(8,128)S(1)} %get-tuple-element.371) | copy-start | bytes 393220
  174.7 6.5 copy-start.4
  174.7 6.5 copy-start.6
  174.7 6.5 copy-start.8
  174.7 6.5 copy-start.9
  208.3 6.6 copy-start.39
  208.3 24.4 %copy-start.40 = (f32[1024]{0:T(1024)S(1)}, f32[1024]{0:T(1024)}, u32[]{:S(2)}) copy-start(f32[1024]{0:T(1024)} %param.25) | copy-start | bytes 12292
  211.0 18.0 %all-to-all-start.1 = ((bf16[4,256,256]{1,2,0:T(8,128)(2,1)}), bf16[4,256,256]{1,2,0:T(8,128)(2,1)S(1)}, u32[]{:S(2)}, u32[]{:S(2)}) async-start(bf16[4,256,256]{1,2,0:T(8,128)(2,1)} %copy.79), calls=%async_computation.1 | async-start | bytes 1048576 | tf_op jit(solution)/shard_map/all_to_all | solution.py:238
  233.1 11.4 copy-start.38
  233.2 11.4 copy-start.42
  246.9 7.0 copy-start.11
  256.5 9.7 copy-start.16
  280.7 4.1 copy-start.18
  283.6 6.6 copy-start.14
  286.5 17.7 %all-to-all-start.2 = ((bf16[256,4,256]{0,2,1:T(8,128)(2,1)}), bf16[256,4,256]{0,2,1:T(8,128)(2,1)S(1)}, u32[]{:S(2)}, u32[]{:S(2)}) async-start(bf16[256,4,256]{0,2,1:T(8,128)(2,1)} %bitcast.276), calls=%async_computation.2 | async-start | bytes 1048576 | tf_op jit(solution)/shard_map/all_to_all | solution.py:276
  308.2 62.1 %copy-start.33 = (f32[2,512,4]{1,0,2:T(2,128)S(1)}, f32[2,512,4]{1,0,2:T(2,128)}, u32[]{:S(2)}) copy-start(f32[2,512,4]{1,0,2:T(2,128)} %copy-done.32) | copy-start | bytes 49156
  308.2 62.1 %copy-start.37 = (f32[4,64]{1,0:T(4,128)S(1)}, f32[4,64]{1,0:T(4,128)}, u32[]{:S(2)}) copy-start(f32[4,64]{1,0:T(4,128)} %copy-done.36) | copy-start | bytes 3076
  317.7 4.8 copy-start.25
  348.8 4.8 copy-start.25
  370.3 6.9 copy-start.5
  370.3 6.9 copy-start.7
  370.3 6.9 copy-start.31
  370.3 6.9 copy-start.35
  380.3 7.3 copy-start.13
  382.9 4.7 copy-start.20
  382.9 6.7 copy-start.17
  382.9 52.4 %all-to-all-start.3 = ((bf16[1024,3,256]{2,1,0:T(4,128)(2,1)}), bf16[1024,3,256]{2,1,0:T(4,128)(2,1)}, u32[]{:S(2)}, u32[]{:S(2)}) async-start(bf16[1024,3,256]{2,1,0:T(4,128)(2,1)} %copy.86), calls=%async_computation.3 | async-start | bytes 4194304 | tf_op jit(solution)/shard_map/all_to_all | solution.py:290
  387.5 1162.0 %all-reduce.19.cloned.1.call-start = ((), (), s32[]{:S(2)}) async-start(), calls=%async_computation.15 | async-start | bytes 67108864
  443.3 1177.4 %reduce-scatter.19.cloned.1.call-start = ((), (), s32[]{:S(2)}) async-start(), calls=%async_computation.12 | async-start | bytes 589824 | tf_op jit(solution)/shard_map/reduce_scatter | solution.py:324
  1552.0 75.6 %reduce-scatter.17.cloned.1.call-start = ((), (), s32[]{:S(2)}) async-start(), calls=%async_computation.11 | async-start | bytes 1769472 | tf_op jit(solution)/shard_map/reduce_scatter | solution.py:324
  1555.4 116.6 %reduce-scatter.23.cloned.1.call-start = ((), (), s32[]{:S(2)}) async-start(), calls=%async_computation.14 | async-start | bytes 2359296 | tf_op jit(solution)/shard_map/reduce_scatter | solution.py:324
  1559.2 167.3 %reduce-scatter.21.cloned.1.call-start = ((), (), s32[]{:S(2)}) async-start(), calls=%async_computation.13 | async-start | bytes 4718592 | tf_op jit(solution)/shard_map/reduce_scatter | solution.py:324
  1564.8 50.1 %copy-start.15 = (f32[256,1024]{1,0:T(8,128)S(1)}, f32[256,1024]{1,0:T(8,128)}, u32[]{:S(2)}) copy-start(f32[256,1024]{1,0:T(8,128)} %copy-done.14) | copy-start | bytes 3145732
  (24 other events, 43.7 us)
Sparse Core Ops, SparseCore 0:
  9.9 38.3 all-gather.3
  50.1 108.6 all-gather.5
  160.7 54.2 all-gather.7
  443.4 1106.0 all-reduce.18
  1553.0 33.0 reduce-scatter.18
  1589.2 38.3 reduce-scatter.16
  1630.9 41.0 reduce-scatter.22
  1675.3 51.1 reduce-scatter.20
